TPU v7x, 32 devices: a whole 2x2x4 slice. The times are simulated.
32 devices in a mesh: group: 2 (over x), tile: 16 (over z, y, core).
Axes of the slice: x: 2, y: 2, z: 4, core: 2. Of those that a mesh axis runs over, the one named last changes fastest.
Arguments:
- hadamard: int32 [128, 1152], P(None, 'tile'), may hold values from -1 to 1, as said below
- stroke: float32 [2304], P(('group', 'tile')), parts along dimension 0, may hold values from 0.3 to 1
- influence: bfloat16 [3, 2304, 8192], P(None, ('group', 'tile')), parts along dimension 1, may hold values from -0.4375 to 0.4375
- amplitude: float32 [1024, 16, 16], P(('group', 'tile')), parts along dimension 0, may hold values from 0.3 to 1
- aberration: float32 [1024, 16, 16], P(('group', 'tile')), parts along dimension 0, may hold values from -3 to 3
- valid_mask: int32 [1024], P(('group', 'tile')), parts along dimension 0, may hold values from 0 to 1, as said below
Outputs:
- imat: float32 [2304, 2, 512], P(('group', 'tile')), parts along dimension 0
There are 2 independent parts, one for each index of `group`. A program takes and returns all parts, laid end to end along the dimension named above; an argument that names none is the same for every part. Nothing has to cross between parts.
Inputs may be any that keep to these rules, and one draw needn't show every extreme that they name: `hadamard`: each column is one column of a Sylvester-Hadamard matrix whose order is the least power of two not below 1152, restricted to 128 distinct rows of it; different actuators take different columns. `valid_mask`: every pupil tile of 32 subapertures holds at least one valid subaperture.
All inputs are finite; a program needn't handle non-finite values.
Results may differ from a plain program's by a relative error of at most 0.0055.
Values may be sent and summed in bfloat16 or wider, within the bound.
A program may use at most 128 MiB of HBM per device.

v0:
```python
import math
import jax
import jax.numpy as jnp
from jax import lax
from jax.sharding import PartitionSpec as P

PIX = 16
HIGHEST = lax.Precision.HIGHEST


def passed_along(value, axis, steps):
    count = lax.axis_size(axis)
    first, last = (max(0, -steps), min(count, count - steps))
    return lax.ppermute(value, axis, [(source, source + steps) for source in range(first, last)])


def shortened(x):
    return jax.tree.map(lambda a: a.astype(jnp.bfloat16) if a.dtype == jnp.float32 else a, x)


def transform_tables(samples, pixels):
    freqs = jnp.arange(pixels, dtype=jnp.float32) - pixels / 2.0
    places = jnp.arange(samples, dtype=jnp.float32)
    angle = 2.0 * jnp.pi * freqs[:, None] * places[None, :] / (2.0 * samples)
    return (jnp.cos(angle), -jnp.sin(angle))


def kron_tables(samples, pixels):
    table_real, table_imag = transform_tables(samples, pixels)
    kron_real = jnp.kron(table_real, table_real) - jnp.kron(table_imag, table_imag)
    kron_imag = jnp.kron(table_real, table_imag) + jnp.kron(table_imag, table_real)
    upper = jnp.concatenate([kron_real.T, kron_imag.T], axis=1)
    lower = jnp.concatenate([-kron_imag.T, kron_real.T], axis=1)
    transform = jnp.concatenate([upper, lower], axis=0)
    centre = jnp.arange(pixels, dtype=jnp.float32) - (pixels - 1) / 2.0
    along_u = jnp.repeat(centre, pixels)
    along_v = jnp.tile(centre, pixels)
    moments = jnp.stack([jnp.ones_like(along_u), along_u, along_v], axis=1)
    return (transform, moments)


def spot_slopes(phase_map, amplitude, aberration, valid_mask):
    patterns, sub_count, samples = (phase_map.shape[0], phase_map.shape[1], phase_map.shape[2])
    flat = samples * samples
    transform, moments = kron_tables(samples, PIX)
    half = PIX * PIX
    phase_rows = phase_map.reshape(patterns, sub_count, flat)
    amp_rows = amplitude.reshape(sub_count, flat)[None]
    abe_rows = aberration.reshape(sub_count, flat)[None]
    results = []
    for pattern_sign in (1.0, -1.0):
        angles = abe_rows + pattern_sign * phase_rows
        field = jnp.concatenate([amp_rows * jnp.cos(angles), amp_rows * jnp.sin(angles)], axis=2)
        focal = jnp.dot(field.reshape(patterns * sub_count, 2 * flat), transform, precision=HIGHEST)
        intensity = focal[:, :half] * focal[:, :half] + focal[:, half:] * focal[:, half:]
        sums = jnp.dot(intensity, moments, precision=HIGHEST)
        centroid_x = sums[:, 1] / sums[:, 0]
        centroid_y = sums[:, 2] / sums[:, 0]
        results.append(
            jnp.stack([centroid_x, centroid_y], axis=1)
            .reshape(patterns, sub_count, 2)
            .transpose(0, 2, 1)
        )
    weights = valid_mask.astype(jnp.float32)[None, None, :]
    return ((results[0] - results[1]) * 0.5 * weights).astype(jnp.bfloat16)


def shape_term(commands, slab):
    term = jnp.dot(commands, slab, preferred_element_type=jnp.float32).astype(jnp.bfloat16)
    return lax.optimization_barrier(term)


def per_device(hadamard, stroke, influence, amplitude, aberration, valid_mask):
    patterns = hadamard.shape[0]
    sub_count = amplitude.shape[0]
    samples = amplitude.shape[1]
    commands = (stroke[None, :] * hadamard.astype(jnp.float32)).astype(jnp.bfloat16)
    local_term = shape_term(commands, influence[1])
    lower_cmds, lower_slab = passed_along((commands, influence[2]), "tile", 1)
    upper_cmds, upper_slab = passed_along((commands, influence[0]), "tile", -1)
    from_lower = shape_term(lower_cmds, lower_slab)
    from_upper = shape_term(upper_cmds, upper_slab)
    phase_map = (
        local_term.astype(jnp.float32)
        + from_lower.astype(jnp.float32)
        + from_upper.astype(jnp.float32)
    )
    block_rows = math.gcd(patterns, 64)
    blocks = phase_map.reshape(patterns // block_rows, block_rows, sub_count, samples, samples)

    def one_block(pattern_block):
        return spot_slopes(pattern_block, amplitude, aberration, valid_mask)

    slopes = lax.map(one_block, blocks).reshape(patterns, 2, sub_count)
    signs_half = hadamard.astype(jnp.bfloat16)
    summed = jnp.einsum(
        "pa,pcs->acs",
        signs_half,
        lax.all_gather(shortened(slopes), "tile", axis=2, tiled=True),
        preferred_element_type=jnp.float32,
    )
    return summed / (patterns * stroke)[:, None, None]


def solution(mesh):
    placed = (
        P(None, "tile"),
        P(("group", "tile")),
        P(None, ("group", "tile"), None),
        P(("group", "tile"), None, None),
        P(("group", "tile"), None, None),
        P(("group", "tile")),
    )
    return jax.shard_map(
        per_device,
        mesh=mesh,
        in_specs=placed,
        out_specs=P(("group", "tile"), None, None),
        check_vma=False,
    )
```

profile of v0, /device:TPU:0, one launch (start us, length us, event | category | flops | bytes accessed | tf_op | source)
XLA Modules:
  0.0 236.9 jit_solution(5249718799039673560)
XLA Ops:
  0.0 2.8 %slice_bitcast_fusion.1 = (bf16[72,8192]{1,0:T(8,128)(2,1)}, bf16[72,8192]{1,0:T(8,128)(2,1)S(1)}) fusion(bf16[3,72,8192]{2,1,0:T(8,128)(2,1)} %param.10), kind=kLoop, calls=%fused_computation.58 | loop fusion | bytes 4718592 | tf_op jit(solution)/shard_map/squeeze | solution.py:79
  2.8 3.6 %collective-permute-start.1 = (bf16[72,8192]{1,0:T(8,128)(2,1)}, bf16[72,8192]{1,0:T(8,128)(2,1)}, u32[]{:S(2)}, u32[]{:S(2)}) collective-permute-start(bf16[72,8192]{1,0:T(8,128)(2,1)} %get-tuple-element.136), channel_id=1, source_target_pairs={{0,1},{1,2},{2,3},{3,4},{4,5},{5,6},{6,7},{7,8},{8,9},{9,10},{10,1... | collective-permute-start | bytes 3538952 | tf_op jit(solution)/shard_map/ppermute | solution.py:14
  7.8 4.1 %collective-permute-start = (bf16[128,72]{0,1:T(8,128)(2,1)S(1)}, bf16[128,72]{0,1:T(8,128)(2,1)S(1)}, u32[]{:S(2)}, u32[]{:S(2)}) collective-permute-start(bf16[128,72]{0,1:T(8,128)(2,1)S(1)} %multiply_convert_fusion), channel_id=1, source_target_pairs={{0,1},{1,2},{2,3},{3,4},{4,5},{5,6},{6,7},{7,8},{8,9},{9,10},{10,1... | collective-permute-start | bytes 55304 | tf_op jit(solution)/shard_map/ppermute | solution.py:14
  19.3 2.8 %convert_add_fusion = f32[128,8192]{1,0:T(8,128)} fusion(bf16[128,8192]{1,0:T(8,128)(2,1)S(1)} %convolution_convert_fusion, bf16[128,8192]{1,0:T(8,128)(2,1)S(1)} %convolution_convert_fusion.1, bf16[128,8192]{1,0:T(8,128)(2,1)S(1)} %convolution_convert_fusion.2), kind=kLoop, calls=%fused_computation.55 | loop fusion | flops 5242880 | bytes 10485760 | tf_op jit(solution)/shard_map/add | solution.py:84
  22.1 5.6 %copy.28 = f32[128,8192]{0,1:T(8,128)} copy(f32[128,8192]{1,0:T(8,128)} %convert_add_fusion) | data formatting | bytes 8388608 | tf_op jit(solution)/shard_map/add | solution.py:84
  27.7 9.2 %reshape.211 = f32[2,64,32,16,16]{1,0,4,3,2:T(2,128)} reshape(f32[128,8192]{0,1:T(8,128)} %copy.28) | data formatting | bytes 8388608 | tf_op jit(solution)/shard_map/reshape | solution.py:89
  36.9 159.1 %while.12 = (s32[]{:T(128)}, bf16[2,64,2,32]{1,0,3,2:T(2,128)(2,1)S(1)}, f32[32,16,16]{0,2,1:T(8,128)S(1)}, f32[32,16,16]{0,2,1:T(8,128)S(1)}, f32[2,64,32,16,16...) while((s32[]{:T(128)}, ...), condition=%wide.region_1.2_spmd, body=%wide.region_0.1_spmd.sunk | while | flops 12933627904 | bytes 64969588 | solution.py:94
  36.9 9.7 %constant_dynamic-slice_fusion.2 = f32[1,64,32,16,16]{1,0,4,3,2:T(1,128)} fusion(f32[2,64,32,16,16]{1,0,4,3,2:T(2,128)} %get-tuple-element.223, s32[]{:T(128)} %get-tuple-element.209), kind=kLoop, calls=%fused_computation.46.clone.1 | loop fusion | bytes 4194308 | tf_op jit(solution)/shard_map/while/body/jit(dynamic_index_in_dim)/dynamic_slice | solution.py:94
  46.6 12.3 %copy.40 = f32[1,64,32,16,16]{2,1,4,3,0:T(8,128)} copy(f32[1,64,32,16,16]{1,0,4,3,2:T(1,128)} %constant_dynamic-slice_fusion.2) | data formatting | bytes 4194304 | tf_op jit(solution)/shard_map/while/body/jit(dynamic_index_in_dim)/dynamic_slice | solution.py:94
  58.9 7.5 %reshape.239 = f32[2048,256]{0,1:T(8,128)} reshape(f32[1,64,32,16,16]{2,1,4,3,0:T(8,128)} %copy.40) | data formatting | bytes 4194304 | tf_op jit(solution)/shard_map/while/body/eval_jaxpr/reshape | solution.py:47
  68.5 16.6 %bitcast_multiply_fusion.5 = (f32[2048,256]{1,0:T(8,128)}, f32[2048,256]{1,0:T(8,128)}, f32[2048,256]{1,0:T(8,128)}, f32[2048,256]{1,0:T(8,128)}) fusion(f32[2048,256]{1,0:T(8,128)S(1)} %copy.41, f32[32,256]{1,0:T(8,128)S(1)} %copy.42, f32[32,256]{1,0:T(8,128)S(1)} %copy.43), kind=kLoop, calls=%fused_computation.3.clone.1 | loop fusion | flops 3670016 | bytes 10551296 | tf_op jit(solution)/shard_map/while/body/eval_jaxpr/mul | solution.py:53
  87.2 2.4 %add.133 = f32[256,256]{1,0:T(8,128)S(1)} reshape(f32[16,16,16,16]{3,2,1,0:T(8,128)} %get-tuple-element.192) | data formatting | bytes 524288 | tf_op jit(solution)/shard_map/while/body/eval_jaxpr/add | solution.py:31
  90.7 9.8 %fusion.57 = f32[2048,512]{1,0:T(8,128)} fusion(f32[2048,256]{1,0:T(8,128)} %get-tuple-element.193, f32[2048,256]{1,0:T(8,128)} %get-tuple-element.194, f32[256,256]{0,1:T(8,128)S(1)} %bitcast.82, f32[256,256]{0,1:T(8,128)S(1)} %bitcast_negate_fusion.2, f32[256,256]{0,1:T(8,128)S(1)} %bitcast.80), kind=kOutput, calls=%fused_computation.8.clone.1 | convolution fusion | flops 6444285952 | bytes 9175040 | tf_op jit(solution)/shard_map/while/body/eval_jaxpr/dot_general | solution.py:54
  100.7 4.4 %fusion.58 = f32[2048,3]{0,1:T(4,128)S(1)} fusion(f32[2048,512]{1,0:T(8,128)} %fusion.57, f32[256,1]{0,1:T(1,128)S(1)} %tile.19, f32[256,1]{0,1:T(1,128)S(1)} %reshape.240, f32[3]{0:T(128)S(1)} %pad.6.clone.2), kind=kOutput, calls=%fused_computation.16.clone.1 | convolution fusion | flops 20448768 | bytes 4220940 | tf_op jit(solution)/shard_map/while/body/eval_jaxpr/dot_general | solution.py:56
  105.1 8.5 %fusion.55 = f32[2048,512]{1,0:T(8,128)S(1)} fusion(f32[2048,256]{1,0:T(8,128)} %get-tuple-element.187, f32[2048,256]{1,0:T(8,128)S(1)} %copy-done, f32[256,256]{0,1:T(8,128)S(1)} %bitcast.83, f32[256,256]{0,1:T(8,128)S(1)} %bitcast_negate_fusion.2, f32[256,256]{0,1:T(8,128)S(1)} %bitcast.81), kind=kOutput, calls=%fused_computation.4.clone.1 | convolution fusion | flops 6444285952 | bytes 9175040 | tf_op jit(solution)/shard_map/while/body/eval_jaxpr/dot_general | solution.py:54
  116.5 9.7 %constant_dynamic-slice_fusion.2 = f32[1,64,32,16,16]{1,0,4,3,2:T(1,128)} fusion(f32[2,64,32,16,16]{1,0,4,3,2:T(2,128)} %get-tuple-element.223, s32[]{:T(128)} %get-tuple-element.209), kind=kLoop, calls=%fused_computation.46.clone.1 | loop fusion | bytes 4194308 | tf_op jit(solution)/shard_map/while/body/jit(dynamic_index_in_dim)/dynamic_slice | solution.py:94
  126.2 12.3 %copy.40 = f32[1,64,32,16,16]{2,1,4,3,0:T(8,128)} copy(f32[1,64,32,16,16]{1,0,4,3,2:T(1,128)} %constant_dynamic-slice_fusion.2) | data formatting | bytes 4194304 | tf_op jit(solution)/shard_map/while/body/jit(dynamic_index_in_dim)/dynamic_slice | solution.py:94
  138.5 7.5 %reshape.239 = f32[2048,256]{0,1:T(8,128)} reshape(f32[1,64,32,16,16]{2,1,4,3,0:T(8,128)} %copy.40) | data formatting | bytes 4194304 | tf_op jit(solution)/shard_map/while/body/eval_jaxpr/reshape | solution.py:47
  148.1 16.6 %bitcast_multiply_fusion.5 = (f32[2048,256]{1,0:T(8,128)}, f32[2048,256]{1,0:T(8,128)}, f32[2048,256]{1,0:T(8,128)}, f32[2048,256]{1,0:T(8,128)}) fusion(f32[2048,256]{1,0:T(8,128)S(1)} %copy.41, f32[32,256]{1,0:T(8,128)S(1)} %copy.42, f32[32,256]{1,0:T(8,128)S(1)} %copy.43), kind=kLoop, calls=%fused_computation.3.clone.1 | loop fusion | flops 3670016 | bytes 10551296 | tf_op jit(solution)/shard_map/while/body/eval_jaxpr/mul | solution.py:53
  166.8 2.4 %add.133 = f32[256,256]{1,0:T(8,128)S(1)} reshape(f32[16,16,16,16]{3,2,1,0:T(8,128)} %get-tuple-element.192) | data formatting | bytes 524288 | tf_op jit(solution)/shard_map/while/body/eval_jaxpr/add | solution.py:31
  170.2 9.8 %fusion.57 = f32[2048,512]{1,0:T(8,128)} fusion(f32[2048,256]{1,0:T(8,128)} %get-tuple-element.193, f32[2048,256]{1,0:T(8,128)} %get-tuple-element.194, f32[256,256]{0,1:T(8,128)S(1)} %bitcast.82, f32[256,256]{0,1:T(8,128)S(1)} %bitcast_negate_fusion.2, f32[256,256]{0,1:T(8,128)S(1)} %bitcast.80), kind=kOutput, calls=%fused_computation.8.clone.1 | convolution fusion | flops 6444285952 | bytes 9175040 | tf_op jit(solution)/shard_map/while/body/eval_jaxpr/dot_general | solution.py:54
  180.3 4.4 %fusion.58 = f32[2048,3]{0,1:T(4,128)S(1)} fusion(f32[2048,512]{1,0:T(8,128)} %fusion.57, f32[256,1]{0,1:T(1,128)S(1)} %tile.19, f32[256,1]{0,1:T(1,128)S(1)} %reshape.240, f32[3]{0:T(128)S(1)} %pad.6.clone.2), kind=kOutput, calls=%fused_computation.16.clone.1 | convolution fusion | flops 20448768 | bytes 4220940 | tf_op jit(solution)/shard_map/while/body/eval_jaxpr/dot_general | solution.py:56
  184.7 8.5 %fusion.55 = f32[2048,512]{1,0:T(8,128)S(1)} fusion(f32[2048,256]{1,0:T(8,128)} %get-tuple-element.187, f32[2048,256]{1,0:T(8,128)S(1)} %copy-done, f32[256,256]{0,1:T(8,128)S(1)} %bitcast.83, f32[256,256]{0,1:T(8,128)S(1)} %bitcast_negate_fusion.2, f32[256,256]{0,1:T(8,128)S(1)} %bitcast.81), kind=kOutput, calls=%fused_computation.4.clone.1 | convolution fusion | flops 6444285952 | bytes 9175040 | tf_op jit(solution)/shard_map/while/body/eval_jaxpr/dot_general | solution.py:54
  196.1 39.6 %all_gather.3 = bf16[128,2,512]{0,2,1:T(8,128)(2,1)S(1)} all-gather(bf16[128,2,32]{0,2,1:T(8,128)(2,1)S(1)} %reshape.212), channel_id=1, replica_groups=mesh['group'=2,'tile'=16] {'tile'}, dimensions={2}, use_global_device_ids=true | all-gather | bytes 278528 | tf_op jit(solution)/shard_map/all_gather | solution.py:99
  (78 shorter events, 26.4 us)
Async XLA Ops:
  0.0 7.7 %copy-start.3 = (s32[128,72]{0,1:T(8,128)S(1)}, s32[128,72]{0,1:T(8,128)}, u32[]{:S(2)}) copy-start(s32[128,72]{0,1:T(8,128)} %param.8) | copy-start | bytes 110596
  0.0 7.7 %copy-start.4 = (f32[72]{0:T(128)S(1)}, f32[72]{0:T(128)}, u32[]{:S(2)}) copy-start(f32[72]{0:T(128)} %param.9) | copy-start | bytes 868
  2.8 12.4 %copy-start.5 = (s32[32]{0:T(128)S(1)}, s32[32]{0:T(128)}, u32[]{:S(2)}) copy-start(s32[32]{0:T(128)} %param.13) | copy-start | bytes 388
  2.8 12.4 %collective-permute-start.1 = (bf16[72,8192]{1,0:T(8,128)(2,1)}, bf16[72,8192]{1,0:T(8,128)(2,1)}, u32[]{:S(2)}, u32[]{:S(2)}) collective-permute-start(bf16[72,8192]{1,0:T(8,128)(2,1)} %get-tuple-element.136), channel_id=1, source_target_pairs={{0,1},{1,2},{2,3},{3,4},{4,5},{5,6},{6,7},{7,8},{8,9},{9,10},{10,1... | collective-permute-start | bytes 3538952 | tf_op jit(solution)/shard_map/ppermute | solution.py:14
  6.4 10.9 %collective-permute-start.3 = (bf16[72,8192]{1,0:T(8,128)(2,1)S(1)}, bf16[72,8192]{1,0:T(8,128)(2,1)}, u32[]{:S(2)}, u32[]{:S(2)}) collective-permute-start(bf16[72,8192]{1,0:T(8,128)(2,1)S(1)} %get-tuple-element.137), channel_id=1, source_target_pairs={{1,0},{2,1},{3,2},{4,3},{5,4},{6,5},{7,6},{8,7},{9,8},{10,9},{11,1... | collective-permute-start | bytes 3538952 | tf_op jit(solution)/shard_map/ppermute | solution.py:14
  7.8 7.5 %collective-permute-start = (bf16[128,72]{0,1:T(8,128)(2,1)S(1)}, bf16[128,72]{0,1:T(8,128)(2,1)S(1)}, u32[]{:S(2)}, u32[]{:S(2)}) collective-permute-start(bf16[128,72]{0,1:T(8,128)(2,1)S(1)} %multiply_convert_fusion), channel_id=1, source_target_pairs={{0,1},{1,2},{2,3},{3,4},{4,5},{5,6},{6,7},{7,8},{8,9},{9,10},{10,1... | collective-permute-start | bytes 55304 | tf_op jit(solution)/shard_map/ppermute | solution.py:14
  11.9 5.4 %collective-permute-start.2 = (bf16[128,72]{0,1:T(8,128)(2,1)S(1)}, bf16[128,72]{0,1:T(8,128)(2,1)S(1)}, u32[]{:S(2)}, u32[]{:S(2)}) collective-permute-start(bf16[128,72]{0,1:T(8,128)(2,1)S(1)} %multiply_convert_fusion), channel_id=1, source_target_pairs={{1,0},{2,1},{3,2},{4,3},{5,4},{6,5},{7,6},{8,7},{9,8},{10,9},{11,1... | collective-permute-start | bytes 55304 | tf_op jit(solution)/shard_map/ppermute | solution.py:14
  27.7 9.2 %copy-start.1 = (f32[32,16,16]{0,2,1:T(8,128)S(1)}, f32[32,16,16]{0,2,1:T(8,128)}, u32[]{:S(2)}) copy-start(f32[32,16,16]{0,2,1:T(8,128)} %param.11) | copy-start | bytes 98308
  27.7 9.2 %copy-start.2 = (f32[32,16,16]{0,2,1:T(8,128)S(1)}, f32[32,16,16]{0,2,1:T(8,128)}, u32[]{:S(2)}) copy-start(f32[32,16,16]{0,2,1:T(8,128)} %param.12) | copy-start | bytes 98308
  100.5 4.7 %copy-start = (f32[2048,256]{1,0:T(8,128)S(1)}, f32[2048,256]{1,0:T(8,128)}, u32[]{:S(2)}) copy-start(f32[2048,256]{1,0:T(8,128)} %get-tuple-element.188) | copy-start | bytes 6291460 | tf_op jit(solution)/shard_map/while
  180.0 4.7 %copy-start = (f32[2048,256]{1,0:T(8,128)S(1)}, f32[2048,256]{1,0:T(8,128)}, u32[]{:S(2)}) copy-start(f32[2048,256]{1,0:T(8,128)} %get-tuple-element.188) | copy-start | bytes 6291460 | tf_op jit(solution)/shard_map/while
where the time goes:
time: 238 us; the launch traced here: 237 us
  local copies, waits for them, and re-layouts  90.3 us (38%)
  matrix products  55.7 us (23%)
  other arithmetic  40.7 us (17%)
  blocking collectives  39.6 us (17%)
  starting transfers between devices  10.3 us (4%)
    dynamic_slice x4, local copies, waits for them, and re-layouts, per_device(): slopes = lax.map(one_block, blocks).reshape(patterns, 2, sub_count)  44.1 us
    all_gather x1, blocking collectives, per_device(): lax.all_gather(shortened(slopes), 'tile', axis=2, tiled=True)  39.6 us
    dot_general x4, matrix products, spot_slopes(): jnp.dot(field.reshape(patterns * sub_count, 2 * flat), transform, precisi...  36.6 us
    mul x2, other arithmetic, spot_slopes(): amp_rows * jnp.cos(angles)  33.3 us
    reshape x4, local copies, waits for them, and re-layouts, spot_slopes(): phase_rows = phase_map.reshape(patterns, sub_count, flat)  18.8 us
    dot_general x4, matrix products, spot_slopes(): sums = jnp.dot(intensity, moments, precision=HIGHEST)  12.9 us
    ppermute x4, starting transfers between devices, passed_along(): lax.ppermute(value, axis, [(source, source + steps) for source in range(f...  10.3 us
    reshape x1, local copies, waits for them, and re-layouts, per_device(): phase_map.reshape(patterns // block_rows, block_rows, sub_count, samples,...  9.2 us
  transfers between devices with their start and end apart: 4, of which 0 were waited for; matrix products, arithmetic and copies ran while one was open for 2% of the time, Pallas kernels for 0%

commit v1 on v0

--- a/solution.py
+++ b/solution.py
@@ -6,6 +6,35 @@
 
 PIX = 16
 HIGHEST = lax.Precision.HIGHEST
+
+
+def group_strips_all(mine):
+    w2 = lax.axis_size("tile")
+    r2 = lax.axis_index("tile")
+    built, new, piece_now = (w2, r2, mine.shape[2])
+    views = []
+    for j0, b in enumerate(mine.shape):
+        views.append(b * built if j0 == 2 else b)
+    row_out = jnp.zeros(views, mine.dtype)
+    reply = lax.dynamic_update_slice_in_dim(row_out, mine, new * piece_now, axis=2)
+    y_new = earlier = mine
+    for kk in tuple(range(1, built // 2 + 1)):
+        entries = []
+        for j0 in tuple(range(built)):
+            entries.append((j0, (j0 + 1) % built))
+        y_new = lax.ppermute(y_new, "tile", entries)
+        reply = lax.dynamic_update_slice_in_dim(
+            reply, y_new, (new - kk) % built * piece_now, axis=2
+        )
+        if 2 * kk < built:
+            in_order = []
+            for j0 in [*range(built)]:
+                in_order.append((j0, (j0 - 1) % built))
+            earlier = lax.ppermute(earlier, "tile", in_order)
+            reply = lax.dynamic_update_slice_in_dim(
+                reply, earlier, (new + kk) % built * piece_now, axis=2
+            )
+    return reply
 
 
 def passed_along(value, axis, steps):
@@ -96,7 +125,7 @@
     summed = jnp.einsum(
         "pa,pcs->acs",
         signs_half,
-        lax.all_gather(shortened(slopes), "tile", axis=2, tiled=True),
+        group_strips_all(shortened(slopes)),
         preferred_element_type=jnp.float32,
     )
     return summed / (patterns * stroke)[:, None, None]

time: 238 us -> 287 us (1.21); the launches traced: 237 us -> 282 us
  starting transfers between devices: 10.3 us -> 56.5 us
  blocking collectives: 39.6 us -> 0 us
  loops' own time: 0.19 us -> 16.9 us
  local copies, waits for them, and re-layouts: 90.3 us -> 102 us
  waiting for transfers between devices: 0.01 us -> 8.94 us
    ppermute x0 -> x15, starting transfers between devices: none -> 46.3 us  [the longest x7 24.6 us: group_strips_all(): earlier = lax.ppermute(earlier, 'tile', in_order)]
    all_gather x1 -> x0, blocking collectives: 39.6 us -> none  [per_device(): lax.all_gather(shortened(slopes), 'tile', axis=2, tiled=True)]
    another operation x1, loops' own time: 0.19 us -> 16.9 us  [per_device(): slopes = lax.map(one_block, blocks).reshape(patterns, 2, sub_count)]
    dynamic_update_slice x0 -> x16, local copies, waits for them, and re-layouts: none -> 9.76 us  [the longest x8 4.79 us: group_strips_all(): lax.dynamic_update_slice_in_dim(reply, y_new, (new - kk) % built * piece_...]
    ppermute x0 -> x15, waiting for transfers between devices: none -> 8.93 us  [the longest x8 6.12 us: group_strips_all(): y_new = lax.ppermute(y_new, 'tile', entries)]
  transfers between devices with their start and end apart: 4 -> 19, of which waited for: 0 -> 12; matrix products, arithmetic and copies ran while one was open for 2% -> 5% of each run, Pallas kernels for 0% -> 0%
where the time goes in v1:
time: 287 us; the launch traced here: 282 us
  local copies, waits for them, and re-layouts  102 us (36%)
  starting transfers between devices  56.5 us (20%)
  matrix products  55.7 us (19%)
  other arithmetic  40.7 us (14%)
  loops' own time  16.9 us (6%)
  waiting for transfers between devices  8.94 us (3%)
    dynamic_slice x4, local copies, waits for them, and re-layouts, per_device(): slopes = lax.map(one_block, blocks).reshape(patterns, 2, sub_count)  44.1 us
    dot_general x4, matrix products, spot_slopes(): jnp.dot(field.reshape(patterns * sub_count, 2 * flat), transform, precisi...  36.6 us
    mul x2, other arithmetic, spot_slopes(): amp_rows * jnp.cos(angles)  33.1 us
    ppermute x7, starting transfers between devices, group_strips_all(): earlier = lax.ppermute(earlier, 'tile', in_order)  24.6 us
    ppermute x8, starting transfers between devices, group_strips_all(): y_new = lax.ppermute(y_new, 'tile', entries)  21.7 us
    reshape x4, local copies, waits for them, and re-layouts, spot_slopes(): phase_rows = phase_map.reshape(patterns, sub_count, flat)  18.9 us
    another operation x1, loops' own time, per_device(): slopes = lax.map(one_block, blocks).reshape(patterns, 2, sub_count)  16.9 us
    dot_general x4, matrix products, spot_slopes(): sums = jnp.dot(intensity, moments, precision=HIGHEST)  12.9 us
  transfers between devices with their start and end apart: 19, of which 12 were waited for; matrix products, arithmetic and copies ran while one was open for 5% of the time, Pallas kernels for 0%

profile of v1, /device:TPU:0, one launch (start us, length us, event | category | flops | bytes accessed | tf_op | source)
XLA Modules:
  0.0 281.6 jit_solution(12435528621674730928)
XLA Ops:
  7.8 4.1 %collective-permute-start = (bf16[128,72]{0,1:T(8,128)(2,1)S(1)}, bf16[128,72]{0,1:T(8,128)(2,1)S(1)}, u32[]{:S(2)}, u32[]{:S(2)}) collective-permute-start(bf16[128,72]{0,1:T(8,128)(2,1)S(1)} %multiply_convert_fusion), channel_id=1, source_target_pairs={{0,1},{1,2},{2,3},{3,4},{4,5},{5,6},{6,7},{7,8},{8,9},{9,10},{10,1... | collective-permute-start | bytes 55304 | tf_op jit(solution)/shard_map/ppermute | solution.py:43
  22.2 5.6 %copy.59 = f32[128,8192]{0,1:T(8,128)} copy(f32[128,8192]{1,0:T(8,128)} %convert_add_fusion) | data formatting | bytes 8388608 | tf_op jit(solution)/shard_map/add | solution.py:113
  27.8 9.3 %reshape.211 = f32[2,64,32,16,16]{1,0,4,3,2:T(2,128)} reshape(f32[128,8192]{0,1:T(8,128)} %copy.59) | data formatting | bytes 8388608 | tf_op jit(solution)/shard_map/reshape | solution.py:118
  37.0 175.8 %while.12 = (s32[]{:T(128)}, bf16[2,64,2,32]{1,0,3,2:T(2,128)(2,1)S(1)}, f32[32,16,16]{0,2,1:T(8,128)S(1)}, f32[32,16,16]{0,2,1:T(8,128)S(1)}, f32[2,64,32,16,16...) while((s32[]{:T(128)}, ...), condition=%wide.region_1.2_spmd, body=%wide.region_0.1_spmd.sunk | while | flops 12933627904 | bytes 64969588 | solution.py:123
  53.5 9.7 %constant_dynamic-slice_fusion.2 = f32[1,64,32,16,16]{1,0,4,3,2:T(1,128)} fusion(f32[2,64,32,16,16]{1,0,4,3,2:T(2,128)} %get-tuple-element.223, s32[]{:T(128)} %get-tuple-element.209), kind=kLoop, calls=%fused_computation.46.clone.1 | loop fusion | bytes 4194308 | tf_op jit(solution)/shard_map/while/body/jit(dynamic_index_in_dim)/dynamic_slice | solution.py:123
  63.3 12.3 %copy.87 = f32[1,64,32,16,16]{2,1,4,3,0:T(8,128)} copy(f32[1,64,32,16,16]{1,0,4,3,2:T(1,128)} %constant_dynamic-slice_fusion.2) | data formatting | bytes 4194304 | tf_op jit(solution)/shard_map/while/body/jit(dynamic_index_in_dim)/dynamic_slice | solution.py:123
  75.6 7.5 %reshape.239 = f32[2048,256]{0,1:T(8,128)} reshape(f32[1,64,32,16,16]{2,1,4,3,0:T(8,128)} %copy.87) | data formatting | bytes 4194304 | tf_op jit(solution)/shard_map/while/body/eval_jaxpr/reshape | solution.py:76
  85.1 16.6 %bitcast_multiply_fusion.5 = (f32[2048,256]{1,0:T(8,128)}, f32[2048,256]{1,0:T(8,128)}, f32[2048,256]{1,0:T(8,128)}, f32[2048,256]{1,0:T(8,128)}) fusion(f32[2048,256]{1,0:T(8,128)S(1)} %copy.88, f32[32,256]{1,0:T(8,128)S(1)} %copy.89, f32[32,256]{1,0:T(8,128)S(1)} %copy.90), kind=kLoop, calls=%fused_computation.3.clone.1 | loop fusion | flops 3670016 | bytes 10551296 | tf_op jit(solution)/shard_map/while/body/eval_jaxpr/mul | solution.py:82
  107.3 9.8 %fusion.57 = f32[2048,512]{1,0:T(8,128)} fusion(f32[2048,256]{1,0:T(8,128)} %get-tuple-element.193, f32[2048,256]{1,0:T(8,128)} %get-tuple-element.194, f32[256,256]{0,1:T(8,128)S(1)} %bitcast.82, f32[256,256]{0,1:T(8,128)S(1)} %bitcast_negate_fusion.2, f32[256,256]{0,1:T(8,128)S(1)} %bitcast.80), kind=kOutput, calls=%fused_computation.8.clone.1 | convolution fusion | flops 6444285952 | bytes 9175040 | tf_op jit(solution)/shard_map/while/body/eval_jaxpr/dot_general | solution.py:83
  117.4 4.4 %fusion.58 = f32[2048,3]{0,1:T(4,128)S(1)} fusion(f32[2048,512]{1,0:T(8,128)} %fusion.57, f32[256,1]{0,1:T(1,128)S(1)} %tile.19, f32[256,1]{0,1:T(1,128)S(1)} %reshape.240, f32[3]{0:T(128)S(1)} %pad.6.clone.2), kind=kOutput, calls=%fused_computation.16.clone.1 | convolution fusion | flops 20448768 | bytes 4220940 | tf_op jit(solution)/shard_map/while/body/eval_jaxpr/dot_general | solution.py:85
  121.8 8.5 %fusion.55 = f32[2048,512]{1,0:T(8,128)S(1)} fusion(f32[2048,256]{1,0:T(8,128)} %get-tuple-element.187, f32[2048,256]{1,0:T(8,128)S(1)} %copy-done, f32[256,256]{0,1:T(8,128)S(1)} %bitcast.83, f32[256,256]{0,1:T(8,128)S(1)} %bitcast_negate_fusion.2, f32[256,256]{0,1:T(8,128)S(1)} %bitcast.81), kind=kOutput, calls=%fused_computation.4.clone.1 | convolution fusion | flops 6444285952 | bytes 9175040 | tf_op jit(solution)/shard_map/while/body/eval_jaxpr/dot_general | solution.py:83
  133.1 9.7 %constant_dynamic-slice_fusion.2 = f32[1,64,32,16,16]{1,0,4,3,2:T(1,128)} fusion(f32[2,64,32,16,16]{1,0,4,3,2:T(2,128)} %get-tuple-element.223, s32[]{:T(128)} %get-tuple-element.209), kind=kLoop, calls=%fused_computation.46.clone.1 | loop fusion | bytes 4194308 | tf_op jit(solution)/shard_map/while/body/jit(dynamic_index_in_dim)/dynamic_slice | solution.py:123
  142.8 12.3 %copy.87 = f32[1,64,32,16,16]{2,1,4,3,0:T(8,128)} copy(f32[1,64,32,16,16]{1,0,4,3,2:T(1,128)} %constant_dynamic-slice_fusion.2) | data formatting | bytes 4194304 | tf_op jit(solution)/shard_map/while/body/jit(dynamic_index_in_dim)/dynamic_slice | solution.py:123
  155.1 7.5 %reshape.239 = f32[2048,256]{0,1:T(8,128)} reshape(f32[1,64,32,16,16]{2,1,4,3,0:T(8,128)} %copy.87) | data formatting | bytes 4194304 | tf_op jit(solution)/shard_map/while/body/eval_jaxpr/reshape | solution.py:76
  164.7 16.6 %bitcast_multiply_fusion.5 = (f32[2048,256]{1,0:T(8,128)}, f32[2048,256]{1,0:T(8,128)}, f32[2048,256]{1,0:T(8,128)}, f32[2048,256]{1,0:T(8,128)}) fusion(f32[2048,256]{1,0:T(8,128)S(1)} %copy.88, f32[32,256]{1,0:T(8,128)S(1)} %copy.89, f32[32,256]{1,0:T(8,128)S(1)} %copy.90), kind=kLoop, calls=%fused_computation.3.clone.1 | loop fusion | flops 3670016 | bytes 10551296 | tf_op jit(solution)/shard_map/while/body/eval_jaxpr/mul | solution.py:82
  186.9 9.8 %fusion.57 = f32[2048,512]{1,0:T(8,128)} fusion(f32[2048,256]{1,0:T(8,128)} %get-tuple-element.193, f32[2048,256]{1,0:T(8,128)} %get-tuple-element.194, f32[256,256]{0,1:T(8,128)S(1)} %bitcast.82, f32[256,256]{0,1:T(8,128)S(1)} %bitcast_negate_fusion.2, f32[256,256]{0,1:T(8,128)S(1)} %bitcast.80), kind=kOutput, calls=%fused_computation.8.clone.1 | convolution fusion | flops 6444285952 | bytes 9175040 | tf_op jit(solution)/shard_map/while/body/eval_jaxpr/dot_general | solution.py:83
  197.0 4.4 %fusion.58 = f32[2048,3]{0,1:T(4,128)S(1)} fusion(f32[2048,512]{1,0:T(8,128)} %fusion.57, f32[256,1]{0,1:T(1,128)S(1)} %tile.19, f32[256,1]{0,1:T(1,128)S(1)} %reshape.240, f32[3]{0:T(128)S(1)} %pad.6.clone.2), kind=kOutput, calls=%fused_computation.16.clone.1 | convolution fusion | flops 20448768 | bytes 4220940 | tf_op jit(solution)/shard_map/while/body/eval_jaxpr/dot_general | solution.py:85
  201.4 8.5 %fusion.55 = f32[2048,512]{1,0:T(8,128)S(1)} fusion(f32[2048,256]{1,0:T(8,128)} %get-tuple-element.187, f32[2048,256]{1,0:T(8,128)S(1)} %copy-done, f32[256,256]{0,1:T(8,128)S(1)} %bitcast.83, f32[256,256]{0,1:T(8,128)S(1)} %bitcast_negate_fusion.2, f32[256,256]{0,1:T(8,128)S(1)} %bitcast.81), kind=kOutput, calls=%fused_computation.4.clone.1 | convolution fusion | flops 6444285952 | bytes 9175040 | tf_op jit(solution)/shard_map/while/body/eval_jaxpr/dot_general | solution.py:83
  213.0 19.1 %collective-permute-start.4 = (bf16[128,2,32]{0,2,1:T(8,128)(2,1)S(1)}, bf16[128,2,32]{0,2,1:T(8,128)(2,1)S(1)}, u32[]{:S(2)}, u32[]{:S(2)}) collective-permute-start(bf16[128,2,32]{0,2,1:T(8,128)(2,1)S(1)} %reshape.212), channel_id=1, source_target_pairs={{0,1},{1,2},{2,3},{3,4},{4,5},{5,6},{6,7},{7,8},{8,9},{9,10},{10,1... | collective-permute-start | bytes 49160 | tf_op jit(solution)/shard_map/ppermute | solution.py:25
  239.4 4.4 %collective-permute-start.9 = (bf16[128,2,32]{0,2,1:T(8,128)(2,1)S(1)}, bf16[128,2,32]{0,2,1:T(8,128)(2,1)S(1)}, u32[]{:S(2)}, u32[]{:S(2)}) collective-permute-start(bf16[128,2,32]{0,2,1:T(8,128)(2,1)S(1)} %collective-permute-done.7), channel_id=1, source_target_pairs={{0,15},{1,0},{2,1},{3,2},{4,3},{5,4},{6,5},{7,6},{8,7},{9,8},{10,9... | collective-permute-start | bytes 49160 | tf_op jit(solution)/shard_map/ppermute | solution.py:33
  245.3 4.4 %collective-permute-start.11 = (bf16[128,2,32]{0,2,1:T(8,128)(2,1)S(1)}, bf16[128,2,32]{0,2,1:T(8,128)(2,1)S(1)}, u32[]{:S(2)}, u32[]{:S(2)}) collective-permute-start(bf16[128,2,32]{0,2,1:T(8,128)(2,1)S(1)} %collective-permute-done.9), channel_id=1, source_target_pairs={{0,15},{1,0},{2,1},{3,2},{4,3},{5,4},{6,5},{7,6},{8,7},{9,8},{10,9... | collective-permute-start | bytes 49160 | tf_op jit(solution)/shard_map/ppermute | solution.py:33
  251.1 4.4 %collective-permute-start.13 = (bf16[128,2,32]{0,2,1:T(8,128)(2,1)S(1)}, bf16[128,2,32]{0,2,1:T(8,128)(2,1)S(1)}, u32[]{:S(2)}, u32[]{:S(2)}) collective-permute-start(bf16[128,2,32]{0,2,1:T(8,128)(2,1)S(1)} %collective-permute-done.11), channel_id=1, source_target_pairs={{0,15},{1,0},{2,1},{3,2},{4,3},{5,4},{6,5},{7,6},{8,7},{9,8},{10,9... | collective-permute-start | bytes 49160 | tf_op jit(solution)/shard_map/ppermute | solution.py:33
  257.0 4.4 %collective-permute-start.15 = (bf16[128,2,32]{0,2,1:T(8,128)(2,1)S(1)}, bf16[128,2,32]{0,2,1:T(8,128)(2,1)S(1)}, u32[]{:S(2)}, u32[]{:S(2)}) collective-permute-start(bf16[128,2,32]{0,2,1:T(8,128)(2,1)S(1)} %collective-permute-done.13), channel_id=1, source_target_pairs={{0,15},{1,0},{2,1},{3,2},{4,3},{5,4},{6,5},{7,6},{8,7},{9,8},{10,9... | collective-permute-start | bytes 49160 | tf_op jit(solution)/shard_map/ppermute | solution.py:33
  262.9 4.4 %collective-permute-start.17 = (bf16[128,2,32]{0,2,1:T(8,128)(2,1)S(1)}, bf16[128,2,32]{0,2,1:T(8,128)(2,1)S(1)}, u32[]{:S(2)}, u32[]{:S(2)}) collective-permute-start(bf16[128,2,32]{0,2,1:T(8,128)(2,1)S(1)} %collective-permute-done.15), channel_id=1, source_target_pairs={{0,15},{1,0},{2,1},{3,2},{4,3},{5,4},{6,5},{7,6},{8,7},{9,8},{10,9... | collective-permute-start | bytes 49160 | tf_op jit(solution)/shard_map/ppermute | solution.py:33
  (140 shorter events, 66.2 us)
Async XLA Ops:
  0.0 7.7 %copy-start.3 = (s32[128,72]{0,1:T(8,128)S(1)}, s32[128,72]{0,1:T(8,128)}, u32[]{:S(2)}) copy-start(s32[128,72]{0,1:T(8,128)} %param.8) | copy-start | bytes 110596
  0.0 7.7 %copy-start.4 = (f32[72]{0:T(128)S(1)}, f32[72]{0:T(128)}, u32[]{:S(2)}) copy-start(f32[72]{0:T(128)} %param.9) | copy-start | bytes 868
  2.9 12.4 %copy-start.5 = (s32[32]{0:T(128)S(1)}, s32[32]{0:T(128)}, u32[]{:S(2)}) copy-start(s32[32]{0:T(128)} %param.13) | copy-start | bytes 388
  2.9 12.4 %collective-permute-start.1 = (bf16[72,8192]{1,0:T(8,128)(2,1)}, bf16[72,8192]{1,0:T(8,128)(2,1)}, u32[]{:S(2)}, u32[]{:S(2)}) collective-permute-start(bf16[72,8192]{1,0:T(8,128)(2,1)} %get-tuple-element.136), channel_id=1, source_target_pairs={{0,1},{1,2},{2,3},{3,4},{4,5},{5,6},{6,7},{7,8},{8,9},{9,10},{10,1... | collective-permute-start | bytes 3538952 | tf_op jit(solution)/shard_map/ppermute | solution.py:43
  6.4 10.9 %collective-permute-start.3 = (bf16[72,8192]{1,0:T(8,128)(2,1)S(1)}, bf16[72,8192]{1,0:T(8,128)(2,1)}, u32[]{:S(2)}, u32[]{:S(2)}) collective-permute-start(bf16[72,8192]{1,0:T(8,128)(2,1)S(1)} %get-tuple-element.137), channel_id=1, source_target_pairs={{1,0},{2,1},{3,2},{4,3},{5,4},{6,5},{7,6},{8,7},{9,8},{10,9},{11,1... | collective-permute-start | bytes 3538952 | tf_op jit(solution)/shard_map/ppermute | solution.py:43
  7.8 7.5 %collective-permute-start = (bf16[128,72]{0,1:T(8,128)(2,1)S(1)}, bf16[128,72]{0,1:T(8,128)(2,1)S(1)}, u32[]{:S(2)}, u32[]{:S(2)}) collective-permute-start(bf16[128,72]{0,1:T(8,128)(2,1)S(1)} %multiply_convert_fusion), channel_id=1, source_target_pairs={{0,1},{1,2},{2,3},{3,4},{4,5},{5,6},{6,7},{7,8},{8,9},{9,10},{10,1... | collective-permute-start | bytes 55304 | tf_op jit(solution)/shard_map/ppermute | solution.py:43
  12.0 5.4 %collective-permute-start.2 = (bf16[128,72]{0,1:T(8,128)(2,1)S(1)}, bf16[128,72]{0,1:T(8,128)(2,1)S(1)}, u32[]{:S(2)}, u32[]{:S(2)}) collective-permute-start(bf16[128,72]{0,1:T(8,128)(2,1)S(1)} %multiply_convert_fusion), channel_id=1, source_target_pairs={{1,0},{2,1},{3,2},{4,3},{5,4},{6,5},{7,6},{8,7},{9,8},{10,9},{11,1... | collective-permute-start | bytes 55304 | tf_op jit(solution)/shard_map/ppermute | solution.py:43
  27.8 9.3 %copy-start.1 = (f32[32,16,16]{0,2,1:T(8,128)S(1)}, f32[32,16,16]{0,2,1:T(8,128)}, u32[]{:S(2)}) copy-start(f32[32,16,16]{0,2,1:T(8,128)} %param.11) | copy-start | bytes 98308
  27.8 9.3 %copy-start.2 = (f32[32,16,16]{0,2,1:T(8,128)S(1)}, f32[32,16,16]{0,2,1:T(8,128)}, u32[]{:S(2)}) copy-start(f32[32,16,16]{0,2,1:T(8,128)} %param.12) | copy-start | bytes 98308
  213.0 20.0 %collective-permute-start.4 = (bf16[128,2,32]{0,2,1:T(8,128)(2,1)S(1)}, bf16[128,2,32]{0,2,1:T(8,128)(2,1)S(1)}, u32[]{:S(2)}, u32[]{:S(2)}) collective-permute-start(bf16[128,2,32]{0,2,1:T(8,128)(2,1)S(1)} %reshape.212), channel_id=1, source_target_pairs={{0,1},{1,2},{2,3},{3,4},{4,5},{5,6},{6,7},{7,8},{8,9},{9,10},{10,1... | collective-permute-start | bytes 49160 | tf_op jit(solution)/shard_map/ppermute | solution.py:25
  232.1 3.3 %collective-permute-start.5 = (bf16[128,2,32]{0,2,1:T(8,128)(2,1)S(1)}, bf16[128,2,32]{0,2,1:T(8,128)(2,1)S(1)}, u32[]{:S(2)}, u32[]{:S(2)}) collective-permute-start(bf16[128,2,32]{0,2,1:T(8,128)(2,1)S(1)} %reshape.212), channel_id=1, source_target_pairs={{0,15},{1,0},{2,1},{3,2},{4,3},{5,4},{6,5},{7,6},{8,7},{9,8},{10,9... | collective-permute-start | bytes 49160 | tf_op jit(solution)/shard_map/ppermute | solution.py:33
  232.9 5.9 %collective-permute-start.6 = (bf16[128,2,32]{0,2,1:T(8,128)(2,1)S(1)}, bf16[128,2,32]{0,2,1:T(8,128)(2,1)S(1)}, u32[]{:S(2)}, u32[]{:S(2)}) collective-permute-start(bf16[128,2,32]{0,2,1:T(8,128)(2,1)S(1)} %collective-permute-done.4), channel_id=1, source_target_pairs={{0,1},{1,2},{2,3},{3,4},{4,5},{5,6},{6,7},{7,8},{8,9},{9,10},{10,1... | collective-permute-start | bytes 49160 | tf_op jit(solution)/shard_map/ppermute | solution.py:25
  235.4 4.0 %collective-permute-start.7 = (bf16[128,2,32]{0,2,1:T(8,128)(2,1)S(1)}, bf16[128,2,32]{0,2,1:T(8,128)(2,1)S(1)}, u32[]{:S(2)}, u32[]{:S(2)}) collective-permute-start(bf16[128,2,32]{0,2,1:T(8,128)(2,1)S(1)} %collective-permute-done.5), channel_id=1, source_target_pairs={{0,15},{1,0},{2,1},{3,2},{4,3},{5,4},{6,5},{7,6},{8,7},{9,8},{10,9... | collective-permute-start | bytes 49160 | tf_op jit(solution)/shard_map/ppermute | solution.py:33
  238.8 5.9 %collective-permute-start.8 = (bf16[128,2,32]{0,2,1:T(8,128)(2,1)S(1)}, bf16[128,2,32]{0,2,1:T(8,128)(2,1)S(1)}, u32[]{:S(2)}, u32[]{:S(2)}) collective-permute-start(bf16[128,2,32]{0,2,1:T(8,128)(2,1)S(1)} %collective-permute-done.6), channel_id=1, source_target_pairs={{0,1},{1,2},{2,3},{3,4},{4,5},{5,6},{6,7},{7,8},{8,9},{9,10},{10,1... | collective-permute-start | bytes 49160 | tf_op jit(solution)/shard_map/ppermute | solution.py:25
  239.4 5.9 %collective-permute-start.9 = (bf16[128,2,32]{0,2,1:T(8,128)(2,1)S(1)}, bf16[128,2,32]{0,2,1:T(8,128)(2,1)S(1)}, u32[]{:S(2)}, u32[]{:S(2)}) collective-permute-start(bf16[128,2,32]{0,2,1:T(8,128)(2,1)S(1)} %collective-permute-done.7), channel_id=1, source_target_pairs={{0,15},{1,0},{2,1},{3,2},{4,3},{5,4},{6,5},{7,6},{8,7},{9,8},{10,9... | collective-permute-start | bytes 49160 | tf_op jit(solution)/shard_map/ppermute | solution.py:33
  244.7 5.9 %collective-permute-start.10 = (bf16[128,2,32]{0,2,1:T(8,128)(2,1)S(1)}, bf16[128,2,32]{0,2,1:T(8,128)(2,1)S(1)}, u32[]{:S(2)}, u32[]{:S(2)}) collective-permute-start(bf16[128,2,32]{0,2,1:T(8,128)(2,1)S(1)} %collective-permute-done.8), channel_id=1, source_target_pairs={{0,1},{1,2},{2,3},{3,4},{4,5},{5,6},{6,7},{7,8},{8,9},{9,10},{10,1... | collective-permute-start | bytes 49160 | tf_op jit(solution)/shard_map/ppermute | solution.py:25
  245.3 5.9 %collective-permute-start.11 = (bf16[128,2,32]{0,2,1:T(8,128)(2,1)S(1)}, bf16[128,2,32]{0,2,1:T(8,128)(2,1)S(1)}, u32[]{:S(2)}, u32[]{:S(2)}) collective-permute-start(bf16[128,2,32]{0,2,1:T(8,128)(2,1)S(1)} %collective-permute-done.9), channel_id=1, source_target_pairs={{0,15},{1,0},{2,1},{3,2},{4,3},{5,4},{6,5},{7,6},{8,7},{9,8},{10,9... | collective-permute-start | bytes 49160 | tf_op jit(solution)/shard_map/ppermute | solution.py:33
  250.6 5.9 %collective-permute-start.12 = (bf16[128,2,32]{0,2,1:T(8,128)(2,1)S(1)}, bf16[128,2,32]{0,2,1:T(8,128)(2,1)S(1)}, u32[]{:S(2)}, u32[]{:S(2)}) collective-permute-start(bf16[128,2,32]{0,2,1:T(8,128)(2,1)S(1)} %collective-permute-done.10), channel_id=1, source_target_pairs={{0,1},{1,2},{2,3},{3,4},{4,5},{5,6},{6,7},{7,8},{8,9},{9,10},{10,1... | collective-permute-start | bytes 49160 | tf_op jit(solution)/shard_map/ppermute | solution.py:25
  251.1 5.9 %collective-permute-start.13 = (bf16[128,2,32]{0,2,1:T(8,128)(2,1)S(1)}, bf16[128,2,32]{0,2,1:T(8,128)(2,1)S(1)}, u32[]{:S(2)}, u32[]{:S(2)}) collective-permute-start(bf16[128,2,32]{0,2,1:T(8,128)(2,1)S(1)} %collective-permute-done.11), channel_id=1, source_target_pairs={{0,15},{1,0},{2,1},{3,2},{4,3},{5,4},{6,5},{7,6},{8,7},{9,8},{10,9... | collective-permute-start | bytes 49160 | tf_op jit(solution)/shard_map/ppermute | solution.py:33
  256.4 5.9 %collective-permute-start.14 = (bf16[128,2,32]{0,2,1:T(8,128)(2,1)S(1)}, bf16[128,2,32]{0,2,1:T(8,128)(2,1)S(1)}, u32[]{:S(2)}, u32[]{:S(2)}) collective-permute-start(bf16[128,2,32]{0,2,1:T(8,128)(2,1)S(1)} %collective-permute-done.12), channel_id=1, source_target_pairs={{0,1},{1,2},{2,3},{3,4},{4,5},{5,6},{6,7},{7,8},{8,9},{9,10},{10,1... | collective-permute-start | bytes 49160 | tf_op jit(solution)/shard_map/ppermute | solution.py:25
  257.0 5.9 %collective-permute-start.15 = (bf16[128,2,32]{0,2,1:T(8,128)(2,1)S(1)}, bf16[128,2,32]{0,2,1:T(8,128)(2,1)S(1)}, u32[]{:S(2)}, u32[]{:S(2)}) collective-permute-start(bf16[128,2,32]{0,2,1:T(8,128)(2,1)S(1)} %collective-permute-done.13), channel_id=1, source_target_pairs={{0,15},{1,0},{2,1},{3,2},{4,3},{5,4},{6,5},{7,6},{8,7},{9,8},{10,9... | collective-permute-start | bytes 49160 | tf_op jit(solution)/shard_map/ppermute | solution.py:33
  262.3 5.9 %collective-permute-start.16 = (bf16[128,2,32]{0,2,1:T(8,128)(2,1)S(1)}, bf16[128,2,32]{0,2,1:T(8,128)(2,1)S(1)}, u32[]{:S(2)}, u32[]{:S(2)}) collective-permute-start(bf16[128,2,32]{0,2,1:T(8,128)(2,1)S(1)} %collective-permute-done.14), channel_id=1, source_target_pairs={{0,1},{1,2},{2,3},{3,4},{4,5},{5,6},{6,7},{7,8},{8,9},{9,10},{10,1... | collective-permute-start | bytes 49160 | tf_op jit(solution)/shard_map/ppermute | solution.py:25
  262.9 15.9 %collective-permute-start.17 = (bf16[128,2,32]{0,2,1:T(8,128)(2,1)S(1)}, bf16[128,2,32]{0,2,1:T(8,128)(2,1)S(1)}, u32[]{:S(2)}, u32[]{:S(2)}) collective-permute-start(bf16[128,2,32]{0,2,1:T(8,128)(2,1)S(1)} %collective-permute-done.15), channel_id=1, source_target_pairs={{0,15},{1,0},{2,1},{3,2},{4,3},{5,4},{6,5},{7,6},{8,7},{9,8},{10,9... | collective-permute-start | bytes 49160 | tf_op jit(solution)/shard_map/ppermute | solution.py:33
  268.2 11.5 %collective-permute-start.18 = (bf16[128,2,32]{0,2,1:T(8,128)(2,1)S(1)}, bf16[128,2,32]{0,2,1:T(8,128)(2,1)S(1)}, u32[]{:S(2)}, u32[]{:S(2)}) collective-permute-start(bf16[128,2,32]{0,2,1:T(8,128)(2,1)S(1)} %collective-permute-done.16), channel_id=1, source_target_pairs={{0,1},{1,2},{2,3},{3,4},{4,5},{5,6},{6,7},{7,8},{8,9},{9,10},{10,1... | collective-permute-start | bytes 49160 | tf_op jit(solution)/shard_map/ppermute | solution.py:25
  (2 other events, 9.3 us)
